TPU v7x, 32 devices: a whole 2x2x4 slice. The times are simulated.
32 devices in a mesh: dp: 4 (over y, x), expert: 8 (over z, core).
Axes of the slice: x: 2, y: 2, z: 4, core: 2. Of those that a mesh axis runs over, the one named last changes fastest.
Arguments:
- expert_down: bfloat16 [3072, 2048], P('expert'), may hold values from -0.125 to 0.125
- out_grad: bfloat16 [4096, 2048], P(('dp', 'expert')), parts along dimension 0, may hold values from -6 to 6
- routes: int32 [4096, 2], P(('dp', 'expert')), parts along dimension 0, may hold values from 0 to 3, all different within a row; in each aligned block of 128 rows (0 to 127, 128 to 255, ...) at most 96 rows name the same one
- gates: float32 [4096, 2], P(('dp', 'expert')), parts along dimension 0, may hold values from 0.1 to 1
Outputs:
- hidden_grad: bfloat16 [4096, 2, 768], P(('dp', 'expert')), parts along dimension 0
There are 4 independent parts, one for each index of `dp`. A program takes and returns all parts, laid end to end along the dimension named above; an argument that names none is the same for every part. Nothing has to cross between parts.
Inputs may be any that keep to these rules, and one draw needn't show every extreme that they name: `routes`: each token names 2 different experts; among the 128 tokens of one device no expert is named more than 96 times.
All inputs are finite; a program needn't handle non-finite values.
Results may differ from a plain program's by a relative error of at most 0.0049.
Values may be sent and summed in bfloat16 or wider, within the bound.
No kernel may reach another device: no remote copies, remote signals or barrier semaphores. Data moves between devices by JAX's collectives and lax.ppermute only.
A program may use at most 64 MiB of HBM per device.

v0:
```python
import jax
import jax.numpy as jnp
from jax import lax
from jax.sharding import PartitionSpec as P


def swapped_2(value, axis, apart):
    mask = 2**apart
    pairs = [(source, source ^ mask) for source in range(lax.axis_size(axis))]
    return lax.ppermute(value, axis, pairs)


def slot_table(routes, experts, capacity):
    local_tokens, choices = routes.shape
    expert_ids = routes.reshape(-1)
    one_hot = (expert_ids[:, None] == jnp.arange(experts, dtype=jnp.int32)[None, :]).astype(
        jnp.int32
    )
    earlier = jnp.cumsum(one_hot, axis=0) - one_hot
    slots = jnp.sum(earlier * one_hot, axis=1)
    position = expert_ids * capacity + slots
    source_token = jnp.arange(local_tokens * choices, dtype=jnp.int32) // choices
    token_table = jnp.zeros((experts * capacity,), jnp.int32).at[position].set(source_token)
    return (expert_ids, slots, token_table.reshape(experts, capacity))


def contract_width(rows, weight):
    return lax.dot_general(
        rows, weight, (((2,), (1,)), ((), ())), preferred_element_type=jnp.float32
    )


def shards(expert_down, out_grad, routes, gates):
    devices = lax.axis_size("expert")
    experts = devices // 2
    local_tokens, choices = routes.shape
    hidden_half = expert_down.shape[0]
    capacity = 3 * local_tokens * choices // (2 * experts)
    expert_ids, slots, token_table = slot_table(routes, experts, capacity)
    parity = lax.axis_index("expert") % 2
    swapped = swapped_2(expert_down, "expert", 0)
    first_rows = jnp.where(parity == 0, expert_down, swapped)
    second_rows = jnp.where(parity == 0, swapped, expert_down)
    half_capacity = capacity // 2
    dispatch_order = token_table.reshape(experts, half_capacity, 2).transpose(0, 2, 1)
    outgoing = out_grad[dispatch_order.reshape(devices, half_capacity)]
    arrived = lax.all_to_all(outgoing, "expert", split_axis=0, concat_axis=0, tiled=True)
    low_part = contract_width(arrived, first_rows).astype(jnp.bfloat16)
    high_part = contract_width(arrived, second_rows).astype(jnp.bfloat16)
    product = jnp.concatenate([low_part, high_part], axis=2)
    returned = lax.all_to_all(product, "expert", split_axis=0, concat_axis=0, tiled=True)
    picked = returned.reshape(experts, 2, half_capacity, 2 * hidden_half)[
        expert_ids, slots % 2, slots // 2, :
    ]
    result = (gates.reshape(-1)[:, None] * picked.astype(jnp.float32)).astype(jnp.bfloat16)
    return result.reshape(local_tokens, choices, 2 * hidden_half)


def solution(mesh):
    placed = (
        P("expert", None),
        P(("dp", "expert"), None),
        P(("dp", "expert"), None),
        P(("dp", "expert"), None),
    )
    return jax.shard_map(
        shards,
        mesh=mesh,
        in_specs=placed,
        out_specs=P(("dp", "expert"), None, None),
        check_vma=False,
    )
```

profile of v0, /device:TPU:0, one launch (start us, length us, event | category | flops | bytes accessed | tf_op | source)
XLA Modules:
  0.0 82.3 jit_solution(3519942288194255209)
XLA Ops:
  0.0 0.0 copy-start
  0.0 0.8 %copy.9 = s32[128,2]{1,0:T(8,128)S(1)} copy(s32[128,2]{0,1:T(2,128)} %param.6) | data formatting | bytes 2048 | tf_op args[2]
  0.8 0.1 eq.37
  1.0 0.1 eq.33
  1.1 0.1 reshape.208
  1.3 1.2 %reduce-window.6 = s32[4,2,128]{2,1,0:T(2,128)S(1)} reduce-window(s32[4,2,128]{2,1,0:T(2,128)S(1)} %compare_convert_fusion, s32[]{:T(128)} %constant.54.clone.1), window={size=1x1x128 pad=0_0x0_0x127_0}, to_apply=%region_0.0 | reduce-window | flops 130048 | bytes 8196 | tf_op jit(solution)/shard_map/reduce-window
  2.5 0.1 slice.13
  2.6 0.1 copy.12
  2.7 0.1 copy.13
  2.8 0.1 add_bitcast_fusion
  3.0 1.4 %scatter_custom_fusion = s32[384]{0:T(512)S(1)} fusion(s32[256]{0:T(256)S(1)} %bitcast.46, s32[256]{0:T(256)S(1)} %and_select_fusion.2, s32[]{:T(128)} %constant.54.clone.1), kind=kCustom, calls=%fused_computation.45 | custom fusion | bytes 1540 | tf_op jit(solution)/shard_map/scatter | solution.py:23
  4.4 0.1 reshape_reshape.3
  4.5 0.1 copy.14
  4.6 0.1 reshape.215
  4.7 0.0 copy-done
  4.7 3.1 %gather_fusion = bf16[384,2048]{1,0:T(8,128)(2,1)} fusion(bf16[128,2048]{1,0:T(8,128)(2,1)S(1)} %copy-done, s32[1024]{0:T(1024)S(1)} %pad_clamp_fusion), kind=kCustom, calls=%fused_computation | custom fusion | bytes 3147264 | tf_op jit(solution)/shard_map/gather | solution.py:46
  7.9 6.4 %all-to-all-start = ((bf16[8,48,2048]{2,1,0:T(8,128)(2,1)}), bf16[8,48,2048]{2,1,0:T(8,128)(2,1)S(1)}, u32[]{:S(2)}, u32[]{:S(2)}) async-start(bf16[8,48,2048]{2,1,0:T(8,128)(2,1)} %bitcast.6), calls=%async_computation | async-start | bytes 3145728 | tf_op jit(solution)/shard_map/all_to_all | solution.py:47
  14.2 0.5 collective-permute-start
  14.7 3.5 %collective-permute-done = bf16[384,2048]{1,0:T(8,128)(2,1)} collective-permute-done((bf16[384,2048]{1,0:T(8,128)(2,1)}, bf16[384,2048]{1,0:T(8,128)(2,1)}, u32[]{:S(2)}, u32[]{:S(2)}) %collective-permute-start) | collective-permute-done | bytes 1572896 | tf_op jit(solution)/shard_map/ppermute | solution.py:10
  18.2 33.8 %all-to-all-done = bf16[8,48,2048]{2,1,0:T(8,128)(2,1)S(1)} async-done(((bf16[8,48,2048]{2,1,0:T(8,128)(2,1)}), bf16[8,48,2048]{2,1,0:T(8,128)(2,1)S(1)}, u32[]{:S(2)}, u32[]{:S(2)}) %all-to-all-start) | async-done | bytes 1572896 | tf_op jit(solution)/shard_map/all_to_all | solution.py:47
  52.0 0.0 copy-start.2
  52.0 2.6 %fusion.8 = bf16[8,48,384]{2,1,0:T(8,128)(2,1)S(1)} fusion(bf16[8,48,2048]{2,1,0:T(8,128)(2,1)S(1)} %all-to-all-done, bf16[384,2048]{1,0:T(8,128)(2,1)} %param.4, bf16[384,2048]{1,0:T(8,128)(2,1)} %collective-permute-done, pred[]{:T(512)S(6)} %eq.41), kind=kOutput, calls=%fused_computation.11 | convolution fusion | flops 604913664 | bytes 5013505 | tf_op jit(solution)/shard_map/dot_general | solution.py:28
  54.6 0.0 copy-done.2
  54.6 2.5 %fusion.11 = bf16[8,48,384]{2,1,0:T(8,128)(2,1)S(1)} fusion(bf16[8,48,2048]{2,1,0:T(8,128)(2,1)S(1)} %all-to-all-done, bf16[384,2048]{1,0:T(8,128)(2,1)} %collective-permute-done, bf16[384,2048]{1,0:T(8,128)(2,1)S(1)} %copy-done.2, pred[]{:T(512)S(6)} %eq.41), kind=kOutput, calls=%fused_computation.12 | convolution fusion | flops 604913664 | bytes 5013505 | tf_op jit(solution)/shard_map/dot_general | solution.py:28
  57.1 0.0 copy-start.1
  57.1 0.9 %pad_maximum_fusion = bf16[8,48,768]{2,1,0:T(8,128)(2,1)} fusion(bf16[8,48,384]{2,1,0:T(8,128)(2,1)S(1)} %fusion.11, bf16[8,48,384]{2,1,0:T(8,128)(2,1)S(1)} %fusion.8), kind=kLoop, calls=%fused_computation.14 | loop fusion | flops 1179648 | bytes 1179648 | tf_op jit(solution)/shard_map/concatenate | solution.py:50
  58.0 3.5 %all-to-all-start.1 = ((bf16[8,48,768]{2,1,0:T(8,128)(2,1)}), bf16[8,48,768]{2,1,0:T(8,128)(2,1)S(1)}, u32[]{:S(2)}, u32[]{:S(2)}) async-start(bf16[8,48,768]{2,1,0:T(8,128)(2,1)} %pad_maximum_fusion), calls=%async_computation.1 | async-start | bytes 1179648 | tf_op jit(solution)/shard_map/all_to_all | solution.py:51
  61.5 0.0 copy-done.1
  61.5 0.1 copy.8
  61.6 16.5 %all-to-all-done.1 = bf16[8,48,768]{2,1,0:T(8,128)(2,1)S(1)} async-done(((bf16[8,48,768]{2,1,0:T(8,128)(2,1)}), bf16[8,48,768]{2,1,0:T(8,128)(2,1)S(1)}, u32[]{:S(2)}, u32[]{:S(2)}) %all-to-all-start.1) | async-done | bytes 589856 | tf_op jit(solution)/shard_map/all_to_all | solution.py:51
  78.2 2.7 %gather_fusion.1 = bf16[256,768]{1,0:T(8,128)(2,1)S(1)} fusion(bf16[4,2,48,768]{3,2,1,0:T(8,128)(2,1)S(1)} %bitcast.40, s32[256]{0:T(256)S(1)} %bitcast.41), kind=kCustom, calls=%fused_computation.1 | custom fusion | bytes 789504 | tf_op jit(solution)/shard_map/gather | solution.py:52
  80.8 0.4 reshape.212
  81.2 1.1 %multiply_convert_fusion = bf16[128,2,768]{2,1,0:T(2,128)(2,1)} fusion(f32[128,2,768]{2,1,0:T(2,128)S(1)} %reshape.212, f32[128,2]{1,0:T(8,128)S(1)} %copy.8), kind=kLoop, calls=%fused_computation.13 | loop fusion | flops 393216 | bytes 1180672 | tf_op jit(solution)/shard_map/convert_element_type | solution.py:55
  (8 shorter events, 0.1 us)
Async XLA Ops:
  0.0 4.7 %copy-start = (bf16[128,2048]{1,0:T(8,128)(2,1)S(1)}, bf16[128,2048]{1,0:T(8,128)(2,1)}, u32[]{:S(2)}) copy-start(bf16[128,2048]{1,0:T(8,128)(2,1)} %param.5) | copy-start | bytes 1572868
  7.9 44.2 %all-to-all-start = ((bf16[8,48,2048]{2,1,0:T(8,128)(2,1)}), bf16[8,48,2048]{2,1,0:T(8,128)(2,1)S(1)}, u32[]{:S(2)}, u32[]{:S(2)}) async-start(bf16[8,48,2048]{2,1,0:T(8,128)(2,1)} %bitcast.6), calls=%async_computation | async-start | bytes 3145728 | tf_op jit(solution)/shard_map/all_to_all | solution.py:47
  14.2 4.0 %collective-permute-start = (bf16[384,2048]{1,0:T(8,128)(2,1)}, bf16[384,2048]{1,0:T(8,128)(2,1)}, u32[]{:S(2)}, u32[]{:S(2)}) collective-permute-start(bf16[384,2048]{1,0:T(8,128)(2,1)} %param.4), channel_id=1, source_target_pairs={{0,1},{1,0},{2,3},{3,2},{4,5},{5,4},{6,7},{7,6},{8,9},{9,8},{10,11... | collective-permute-start | bytes 4718600 | tf_op jit(solution)/shard_map/ppermute | solution.py:10
  52.0 2.6 %copy-start.2 = (bf16[384,2048]{1,0:T(8,128)(2,1)S(1)}, bf16[384,2048]{1,0:T(8,128)(2,1)}, u32[]{:S(2)}) copy-start(bf16[384,2048]{1,0:T(8,128)(2,1)} %param.4) | copy-start | bytes 4718596
  57.1 4.4 %copy-start.1 = (f32[128,2]{0,1:T(2,128)S(1)}, f32[128,2]{0,1:T(2,128)}, u32[]{:S(2)}) copy-start(f32[128,2]{0,1:T(2,128)} %param.7) | copy-start | bytes 3076
  58.0 20.2 %all-to-all-start.1 = ((bf16[8,48,768]{2,1,0:T(8,128)(2,1)}), bf16[8,48,768]{2,1,0:T(8,128)(2,1)S(1)}, u32[]{:S(2)}, u32[]{:S(2)}) async-start(bf16[8,48,768]{2,1,0:T(8,128)(2,1)} %pad_maximum_fusion), calls=%async_computation.1 | async-start | bytes 1179648 | tf_op jit(solution)/shard_map/all_to_all | solution.py:51
where the time goes:
time: 82.6 us; the launch traced here: 82.3 us
  waiting for transfers between devices  53.8 us (65%)
  starting transfers between devices  10.4 us (13%)
  local copies, waits for them, and re-layouts  9.58 us (12%)
  matrix products  5.04 us (6%)
  other arithmetic  3.37 us (4%)
    all_to_all x1, waiting for transfers between devices, shards(): lax.all_to_all(outgoing, 'expert', split_axis=0, concat_axis=0, tiled=True)  33.8 us
    all_to_all x1, waiting for transfers between devices, shards(): lax.all_to_all(product, 'expert', split_axis=0, concat_axis=0, tiled=True)  16.5 us
    all_to_all x1, starting transfers between devices, shards(): lax.all_to_all(outgoing, 'expert', split_axis=0, concat_axis=0, tiled=True)  6.35 us
    dot_general x2, matrix products, contract_width(): lax.dot_general(rows, weight, (((2,), (1,)), ((), ())), preferred_element...  5.04 us
    all_to_all x1, starting transfers between devices, shards(): lax.all_to_all(product, 'expert', split_axis=0, concat_axis=0, tiled=True)  3.54 us
    ppermute x1, waiting for transfers between devices, swapped_2(): return lax.ppermute(value, axis, pairs)  3.52 us
    gather x1, local copies, waits for them, and re-layouts, shards(): outgoing = out_grad[dispatch_order.reshape(devices, half_capacity)]  3.13 us
    gather x1, local copies, waits for them, and re-layouts, shards(): returned.reshape(experts, 2, half_capacity, 2 * hidden_half)  2.69 us
  transfers between devices with their start and end apart: 3, of which 3 were waited for; matrix products, arithmetic and copies ran while one was open for 0% of the time, Pallas kernels for 0%

commit v1 on v0

--- a/solution.py
+++ b/solution.py
@@ -1,6 +1,10 @@
+import functools
+
 import jax
 import jax.numpy as jnp
 from jax import lax
+from jax.experimental import pallas as pl
+from jax.experimental.pallas import tpu as pltpu
 from jax.sharding import PartitionSpec as P
 
 
@@ -30,7 +34,7 @@
     )
 
 
-def shards(expert_down, out_grad, routes, gates):
+def slot_shards(expert_down, out_grad, routes, gates):
     devices = lax.axis_size("expert")
     experts = devices // 2
     local_tokens, choices = routes.shape
@@ -56,6 +60,125 @@
     return result.reshape(local_tokens, choices, 2 * hidden_half)
 
 
+VMEM = pltpu.VMEM
+
+
+def project(tokens, low, high):
+    rows = jnp.concatenate([low, high], axis=0)
+    value = lax.dot_general(tokens, rows, (((1,), (1,)), ((), ())), preferred_element_type=jnp.float32)
+    return value.astype(jnp.bfloat16)
+
+
+def keep_chosen(routes, expert, value, kept):
+    choices = routes.shape[1]
+    width = value.shape[1]
+    parts = [
+        jnp.where(routes[:, j : j + 1] == expert, value, kept[:, j * width : (j + 1) * width])
+        for j in range(choices)
+    ]
+    return jnp.concatenate(parts, axis=1)
+
+
+def multiply_body(groups, slots, has_kept, *refs):
+    ids_ref = refs[0]
+    token_refs = refs[1 : 1 + groups]
+    route_refs = refs[1 + groups : 1 + 2 * groups]
+    at = 1 + 2 * groups
+    weight_refs = refs[at : at + 2 * slots]
+    at += 2 * slots
+    kept_refs = refs[at : at + groups] if has_kept else None
+    at += groups if has_kept else 0
+    out_refs = refs[at : at + groups]
+    for g in range(groups):
+        kept = kept_refs[g][...] if has_kept else jnp.zeros(out_refs[g].shape, jnp.bfloat16)
+        for s in range(slots):
+            value = project(token_refs[g][...], weight_refs[2 * s][...], weight_refs[2 * s + 1][...])
+            kept = keep_chosen(route_refs[g][...], ids_ref[s], value, kept)
+        out_refs[g][...] = kept
+
+
+def multiply(ids, tokens, routes, weights, kept=None):
+    groups, slots = len(tokens), len(weights)
+    rows, width = tokens[0].shape
+    piece = weights[0][0].shape[0]
+    choices = routes[0].shape[1]
+    operands = [ids, *tokens, *routes]
+    for low, high in weights:
+        operands += [low, high]
+    if kept is not None:
+        operands += kept
+    shape = jax.ShapeDtypeStruct((rows, choices * 2 * piece), jnp.bfloat16)
+    return pl.pallas_call(
+        functools.partial(multiply_body, groups, slots, kept is not None),
+        out_shape=[shape] * groups,
+        in_specs=[pl.BlockSpec(memory_space=pltpu.SMEM)]
+        + [pl.BlockSpec(memory_space=VMEM)] * (len(operands) - 1),
+        out_specs=[pl.BlockSpec(memory_space=VMEM)] * groups,
+        cost_estimate=pl.CostEstimate(
+            flops=2 * groups * rows * slots * 2 * piece * width,
+            bytes_accessed=2 * (groups * rows * width + slots * 2 * piece * width),
+            transcendentals=0,
+        ),
+        name=f"multiply_{slots}_{'late' if kept is not None else 'early'}",
+    )(*operands)
+
+
+def piece_shards(expert_down, out_grad, routes, gates):
+    devices = lax.axis_size("expert")
+    replicas = lax.axis_size("dp")
+    chips = devices // 2
+    local_tokens, choices = routes.shape
+    hidden_half, width = expert_down.shape
+    piece = hidden_half // replicas
+    replica = lax.axis_index("dp")
+    place = lax.axis_index("expert")
+    chip, core = place // 2, place % 2
+
+    def along(value, by):
+        return lax.ppermute(value, "expert", [(i, (i + 2 * by) % devices) for i in range(devices)])
+
+    def other_core(value):
+        return lax.ppermute(value, "expert", [(i, i ^ 1) for i in range(devices)])
+
+    def other_replica(value, mask):
+        return lax.ppermute(value, "dp", [(i, i ^ mask) for i in range(replicas)])
+
+    mine = lax.dynamic_slice(expert_down, (replica * piece, 0), (piece, width))
+    ups, downs = [mine], [mine]
+    for _ in range(chips // 2):
+        ups.append(along(ups[-1], 1))
+    for _ in range((chips - 1) // 2):
+        downs.append(along(downs[-1], -1))
+    held = [(mine, chip)]
+    for step in range(1, chips // 2 + 1):
+        if step < len(downs):
+            held.append((downs[step], (chip + step) % chips))
+        held.append((ups[step], (chip - step) % chips))
+    weights = [(rows, other_core(rows)) for rows, _ in held]
+    ids = jnp.stack([expert for _, expert in held]).astype(jnp.int32)
+
+    tokens = [out_grad] + [other_replica(out_grad, mask) for mask in range(1, replicas)]
+    named = [routes] + [other_replica(routes, mask) for mask in range(1, replicas)]
+    early = multiply(ids[:-1], tokens, named, weights[:-1])
+    late = multiply(ids[-1:], tokens, named, weights[-1:], early)
+    back = [late[0]] + [other_replica(late[mask], mask) for mask in range(1, replicas)]
+
+    stacked = jnp.stack(back)
+    ordered = stacked[jnp.arange(replicas) ^ replica]
+    ordered = ordered.reshape(replicas, local_tokens, choices, 2, piece)
+    ordered = jnp.where(core == 0, ordered, ordered[:, :, :, ::-1])
+    picked = ordered.transpose(1, 2, 3, 0, 4).reshape(local_tokens, choices, 2 * hidden_half)
+    return (gates[:, :, None] * picked.astype(jnp.float32)).astype(jnp.bfloat16)
+
+
+def shards(expert_down, out_grad, routes, gates):
+    experts, replicas = lax.axis_size("expert") // 2, lax.axis_size("dp")
+    shared = experts <= replicas and replicas & (replicas - 1) == 0
+    shared = shared and expert_down.shape[0] % (16 * replicas) == 0
+    plan = piece_shards if shared else slot_shards
+    return plan(expert_down, out_grad, routes, gates)
+
+
 def solution(mesh):
     placed = (
         P("expert", None),

time: 82.6 us -> 80.8 us (0.978)
  the two profiles are of different devices: /device:TPU:0 before, /device:TPU:16 now
where the time goes in v1:
time: 80.8 us; the launch traced here: 80.6 us
  waiting for transfers between devices  45.5 us (56%)
  starting transfers between devices  17 us (21%)
  Pallas kernels  10.4 us (13%)
  local copies, waits for them, and re-layouts  5.73 us (7%)
  other arithmetic  1.76 us (2%)
    ppermute x9, waiting for transfers between devices, other_replica(): return lax.ppermute(value, 'dp', [(i, i ^ mask) for i in range(replicas)])  30.7 us
    ppermute x3, waiting for transfers between devices, along(): lax.ppermute(value, 'expert', [(i, (i + 2 * by) % devices) for i in range...  14.8 us
    ppermute x9, starting transfers between devices, other_replica(): return lax.ppermute(value, 'dp', [(i, i ^ mask) for i in range(replicas)])  12.5 us
    pallas_call x2, Pallas kernels, multiply(): pl.pallas_call(functools.partial(multiply_body, groups, slots, kept is no...  10.4 us
    ppermute x3, starting transfers between devices, along(): lax.ppermute(value, 'expert', [(i, (i + 2 * by) % devices) for i in range...  3.98 us
    unnamed x19, local copies, waits for them, and re-layouts  3.73 us
  transfers between devices with their start and end apart: 16, of which 8 were waited for; matrix products, arithmetic and copies ran while one was open for 2% of the time, Pallas kernels for 8%

profile of v1, /device:TPU:16, one launch (start us, length us, event | category | flops | bytes accessed | tf_op | source)
XLA Modules:
  0.0 80.6 jit_solution(3688015695511938168)
XLA Ops:
  0.0 0.0 copy-start
  0.0 1.4 %copy-done = bf16[384,2048]{1,0:T(8,128)(2,1)S(1)} copy-done((bf16[384,2048]{1,0:T(8,128)(2,1)S(1)}, bf16[384,2048]{1,0:T(8,128)(2,1)}, u32[]{:S(2)}) %copy-start) | copy-done | bytes 1572888
  1.4 0.0 copy-start.4
  1.5 1.6 %collective-permute-start.6 = (bf16[96,2048]{1,0:T(8,128)(2,1)S(1)}, bf16[96,2048]{1,0:T(8,128)(2,1)}, u32[]{:S(2)}, u32[]{:S(2)}) collective-permute-start(bf16[96,2048]{1,0:T(8,128)(2,1)S(1)} %constant_dynamic-slice_fusion.refs_9_), channel_id=1, source_target_pairs={{0,2},{1,3},{2,4},{3,5},{4,6},{5,7},{6,0},{7,1},{8,10},{9,11},{10,... | collective-permute-start | bytes 1179656 | tf_op jit(solution)/shard_map/ppermute | solution.py:138
  3.1 0.4 collective-permute-start.10
  3.5 1.5 %collective-permute-start = (bf16[128,2048]{1,0:T(8,128)(2,1)}, bf16[128,2048]{1,0:T(8,128)(2,1)S(1)}, u32[]{:S(2)}, u32[]{:S(2)}) collective-permute-start(bf16[128,2048]{1,0:T(8,128)(2,1)} %refs_1_.3), channel_id=1, source_target_pairs={{0,8},{8,0},{16,24},{24,16},{1,9},{9,1},{17,25},{25,17},{2,10},{10... | collective-permute-start | bytes 1572872 | tf_op jit(solution)/shard_map/ppermute | solution.py:144
  5.0 0.0 collective-permute-start.9
  5.0 14.8 %collective-permute-done.6.refs_13_ = bf16[96,2048]{1,0:T(8,128)(2,1)} collective-permute-done((bf16[96,2048]{1,0:T(8,128)(2,1)S(1)}, bf16[96,2048]{1,0:T(8,128)(2,1)}, u32[]{:S(2)}, u32[]{:S(2)}) %collective-permute-start.6) | collective-permute-done | bytes 393248 | tf_op jit(solution)/shard_map/ppermute | solution.py:138
  19.8 1.9 %collective-permute-start.7 = (bf16[96,2048]{1,0:T(8,128)(2,1)}, bf16[96,2048]{1,0:T(8,128)(2,1)}, u32[]{:S(2)}, u32[]{:S(2)}) collective-permute-start(bf16[96,2048]{1,0:T(8,128)(2,1)} %collective-permute-done.6.refs_13_), channel_id=1, source_target_pairs={{0,2},{1,3},{2,4},{3,5},{4,6},{5,7},{6,0},{7,1},{8,10},{9,11},{10,... | collective-permute-start | bytes 1179656 | tf_op jit(solution)/shard_map/ppermute | solution.py:138
  21.7 0.8 copy.16.refs_5_
  22.5 0.0 copy-start.5
  22.5 1.6 %collective-permute-start.3 = (s32[128,2]{1,0:T(8,128)S(1)}, s32[128,2]{1,0:T(8,128)S(1)}, u32[]{:S(2)}, u32[]{:S(2)}) collective-permute-start(s32[128,2]{1,0:T(8,128)S(1)} %copy.16.refs_5_), channel_id=1, source_target_pairs={{0,8},{8,0},{16,24},{24,16},{1,9},{9,1},{17,25},{25,17},{2,10},{10... | collective-permute-start | bytes 3080 | tf_op jit(solution)/shard_map/ppermute | solution.py:144
  24.1 2.8 %collective-permute-done.3.refs_6_ = s32[128,2]{1,0:T(8,128)S(1)} collective-permute-done((s32[128,2]{1,0:T(8,128)S(1)}, s32[128,2]{1,0:T(8,128)S(1)}, u32[]{:S(2)}, u32[]{:S(2)}) %collective-permute-start.3) | collective-permute-done | bytes 1056 | tf_op jit(solution)/shard_map/ppermute | solution.py:144
  26.9 0.0 copy-start.6
  26.9 1.5 %collective-permute-start.4 = (s32[128,2]{1,0:T(8,128)S(1)}, s32[128,2]{1,0:T(8,128)S(1)}, u32[]{:S(2)}, u32[]{:S(2)}) collective-permute-start(s32[128,2]{1,0:T(8,128)S(1)} %copy.16.refs_5_), channel_id=1, source_target_pairs={{0,16},{8,24},{16,0},{24,8},{1,17},{9,25},{17,1},{25,9},{2,18},{10... | collective-permute-start | bytes 3080 | tf_op jit(solution)/shard_map/ppermute | solution.py:144
  28.4 9.1 %collective-permute-done.4.refs_7_ = s32[128,2]{1,0:T(8,128)S(1)} collective-permute-done((s32[128,2]{1,0:T(8,128)S(1)}, s32[128,2]{1,0:T(8,128)S(1)}, u32[]{:S(2)}, u32[]{:S(2)}) %collective-permute-start.4) | collective-permute-done | bytes 1056 | tf_op jit(solution)/shard_map/ppermute | solution.py:144
  37.4 0.0 copy-start.7
  37.4 1.5 %collective-permute-start.5 = (s32[128,2]{1,0:T(8,128)S(1)}, s32[128,2]{1,0:T(8,128)}, u32[]{:S(2)}, u32[]{:S(2)}) collective-permute-start(s32[128,2]{1,0:T(8,128)S(1)} %copy.16.refs_5_), channel_id=1, source_target_pairs={{0,24},{8,16},{16,8},{24,0},{1,25},{9,17},{17,9},{25,1},{2,26},{10... | collective-permute-start | bytes 3080 | tf_op jit(solution)/shard_map/ppermute | solution.py:144
  38.9 0.0 copy-done.5
  38.9 0.0 copy-done.6
  38.9 0.0 copy-done.7
  38.9 3.8 %collective-permute-done.5.refs_8_ = s32[128,2]{1,0:T(8,128)} collective-permute-done((s32[128,2]{1,0:T(8,128)S(1)}, s32[128,2]{1,0:T(8,128)}, u32[]{:S(2)}, u32[]{:S(2)}) %collective-permute-start.5) | collective-permute-done | bytes 1056 | tf_op jit(solution)/shard_map/ppermute | solution.py:144
  42.7 0.5 collective-permute-start.1
  43.3 0.0 collective-permute-done.10.refs_11_
  43.3 2.4 %collective-permute-start.2 = (bf16[128,2048]{1,0:T(8,128)(2,1)}, bf16[128,2048]{1,0:T(8,128)(2,1)S(1)}, u32[]{:S(2)}, u32[]{:S(2)}) collective-permute-start(bf16[128,2048]{1,0:T(8,128)(2,1)} %refs_1_.3), channel_id=1, source_target_pairs={{0,24},{8,16},{16,8},{24,0},{1,25},{9,17},{17,9},{25,1},{2,26},{10... | collective-permute-start | bytes 1572872 | tf_op jit(solution)/shard_map/ppermute | solution.py:144
  45.7 0.0 collective-permute-done.9.refs_10_
  45.7 0.0 collective-permute-start.12
  45.7 0.0 collective-permute-done.refs_2_
  45.7 0.0 copy-start.1
  45.7 0.5 collective-permute-start.11
  46.2 0.0 collective-permute-done.7.refs_9_
  46.2 0.1 collective-permute-start.8
  46.3 0.7 pad_add_fusion.refs_0_
  46.9 10.8 %collective-permute-done.1.refs_3_ = bf16[128,2048]{1,0:T(8,128)(2,1)S(1)} collective-permute-done((bf16[128,2048]{1,0:T(8,128)(2,1)}, bf16[128,2048]{1,0:T(8,128)(2,1)S(1)}, u32[]{:S(2)}, u32[]{:S(2)}) %collective-permute-start.1) | collective-permute-done | bytes 524320 | tf_op jit(solution)/shard_map/ppermute | solution.py:144
  57.7 0.0 copy-start.2
  57.7 0.0 collective-permute-done.2.refs_4_
  57.7 0.0 copy-start.3
  57.7 0.0 collective-permute-done.12.refs_14_
  57.7 0.0 collective-permute-done.11.refs_12_
  57.7 0.0 copy-done.4
  57.8 0.0 copy-done.1
  57.8 0.8 copy-done.2
  58.5 0.2 copy-done.3
  58.8 6.5 %multiply_3_early.1 = (bf16[128,384]{1,0:T(8,128)(2,1)}, bf16[128,384]{1,0:T(8,128)(2,1)}, bf16[128,384]{1,0:T(8,128)(2,1)}, bf16[128,384]{1,0:T(8,128)(2,1)}) custom-call(s32[3]{0:T(128)} %pad_add_fusion.refs_0_, bf16[128,2048]{1,0:T(8,128)(2,1)} %refs_1_.3, bf16[128,2048]{1,0:T(8,128)(2,1)} %copy-done.1, bf16[128,2048]{1,0:T(8,128)(2,1)} %copy-done.2, ...), custom_call_target="tpu_custom_call" | custom-call | flops 1207959552 | bytes 4456448 | tf_op jit(solution)/shard_map/multiply_3_early/pallas_call | solution.py:111
  65.2 0.0 collective-permute-done.8.refs_10_
  65.2 3.9 %multiply_1_late.1 = (bf16[128,384]{1,0:T(8,128)(2,1)}, bf16[128,384]{1,0:T(8,128)(2,1)}, bf16[128,384]{1,0:T(8,128)(2,1)}, bf16[128,384]{1,0:T(8,128)(2,1)}) custom-call(s32[1]{0:T(128)} %bitcast.refs_0_, bf16[128,2048]{1,0:T(8,128)(2,1)} %refs_1_.3, bf16[128,2048]{1,0:T(8,128)(2,1)} %copy-done.1, bf16[128,2048]{1,0:T(8,128)(2,1)} %copy-done.2, ...), custom_call_target="tpu_custom_call" | custom-call | flops 402653184 | bytes 2883584 | tf_op jit(solution)/shard_map/multiply_1_late/pallas_call | solution.py:111
  69.1 1.5 %collective-permute-start.13 = (bf16[128,384]{1,0:T(8,128)(2,1)}, bf16[128,384]{1,0:T(8,128)(2,1)S(1)}, u32[]{:S(2)}, u32[]{:S(2)}) collective-permute-start(bf16[128,384]{1,0:T(8,128)(2,1)} %get-tuple-element.18), channel_id=1, source_target_pairs={{0,8},{8,0},{16,24},{24,16},{1,9},{9,1},{17,25},{25,17},{2,10},{10... | collective-permute-start | bytes 294920 | tf_op jit(solution)/shard_map/ppermute | solution.py:144
  70.6 0.6 collective-permute-start.14
  71.2 1.4 %collective-permute-start.15 = (bf16[128,384]{1,0:T(8,128)(2,1)}, bf16[128,384]{1,0:T(8,128)(2,1)S(1)}, u32[]{:S(2)}, u32[]{:S(2)}) collective-permute-start(bf16[128,384]{1,0:T(8,128)(2,1)} %get-tuple-element.20), channel_id=1, source_target_pairs={{0,24},{8,16},{16,8},{24,0},{1,25},{9,17},{17,9},{25,1},{2,26},{10... | collective-permute-start | bytes 294920 | tf_op jit(solution)/shard_map/ppermute | solution.py:144
  72.6 1.3 %collective-permute-done.13 = bf16[128,384]{1,0:T(8,128)(2,1)S(1)} collective-permute-done((bf16[128,384]{1,0:T(8,128)(2,1)}, bf16[128,384]{1,0:T(8,128)(2,1)S(1)}, u32[]{:S(2)}, u32[]{:S(2)}) %collective-permute-start.13) | collective-permute-done | bytes 98336 | tf_op jit(solution)/shard_map/ppermute | solution.py:144
  74.0 1.5 %collective-permute-done.14 = bf16[128,384]{1,0:T(8,128)(2,1)S(1)} collective-permute-done((bf16[128,384]{1,0:T(8,128)(2,1)}, bf16[128,384]{1,0:T(8,128)(2,1)S(1)}, u32[]{:S(2)}, u32[]{:S(2)}) %collective-permute-start.14) | collective-permute-done | bytes 98336 | tf_op jit(solution)/shard_map/ppermute | solution.py:144
  75.5 1.4 %collective-permute-done.15 = bf16[128,384]{1,0:T(8,128)(2,1)S(1)} collective-permute-done((bf16[128,384]{1,0:T(8,128)(2,1)}, bf16[128,384]{1,0:T(8,128)(2,1)S(1)}, u32[]{:S(2)}, u32[]{:S(2)}) %collective-permute-start.15) | collective-permute-done | bytes 98336 | tf_op jit(solution)/shard_map/ppermute | solution.py:144
  76.9 1.0 %pad_maximum_fusion = bf16[4,128,384]{2,1,0:T(8,128)(2,1)S(1)} fusion(bf16[1,128,384]{2,1,0:T(8,128)(2,1)S(1)} %bitcast.21, bf16[1,128,384]{2,1,0:T(8,128)(2,1)S(1)} %bitcast.20, bf16[1,128,384]{2,1,0:T(8,128)(2,1)S(1)} %bitcast.19, bf16[1,128,384]{2,1,0:T(8,128)(2,1)} %bitcast.18), kind=kLoop, calls=%fused_computation.5 | loop fusion | flops 589824 | bytes 786432 | tf_op jit(solution)/shard_map/stack | solution.py:166
  77.9 0.6 gather_fusion
  78.5 0.2 copy.17
  78.7 0.0 copy-start.8
  78.8 0.1 convert_bitcast_fusion
  78.8 0.1 copy.18
  78.9 0.5 copy-done.8
  79.4 0.1 fusion
  79.5 1.1 %copy.19 = bf16[128,2,768]{2,1,0:T(2,128)(2,1)} copy(bf16[128,2,768]{0,2,1:T(8,128)(2,1)S(1)} %fusion) | data formatting | bytes 786432 | tf_op jit(solution)/shard_map/convert_element_type | solution.py:171
  (3 shorter events, 0.0 us)
Async XLA Ops:
  0.0 1.4 %copy-start = (bf16[384,2048]{1,0:T(8,128)(2,1)S(1)}, bf16[384,2048]{1,0:T(8,128)(2,1)}, u32[]{:S(2)}) copy-start(bf16[384,2048]{1,0:T(8,128)(2,1)} %param.4) | copy-start | bytes 4718596
  1.4 56.3 %copy-start.4 = (bf16[96,2048]{1,0:T(8,128)(2,1)}, bf16[96,2048]{1,0:T(8,128)(2,1)S(1)}, u32[]{:S(2)}) copy-start(bf16[96,2048]{1,0:T(8,128)(2,1)S(1)} %constant_dynamic-slice_fusion.refs_9_) | copy-start | bytes 1179652
  1.5 18.4 %collective-permute-start.6 = (bf16[96,2048]{1,0:T(8,128)(2,1)S(1)}, bf16[96,2048]{1,0:T(8,128)(2,1)}, u32[]{:S(2)}, u32[]{:S(2)}) collective-permute-start(bf16[96,2048]{1,0:T(8,128)(2,1)S(1)} %constant_dynamic-slice_fusion.refs_9_), channel_id=1, source_target_pairs={{0,2},{1,3},{2,4},{3,5},{4,6},{5,7},{6,0},{7,1},{8,10},{9,11},{10,... | collective-permute-start | bytes 1179656 | tf_op jit(solution)/shard_map/ppermute | solution.py:138
  3.1 40.2 %collective-permute-start.10 = (bf16[96,2048]{1,0:T(8,128)(2,1)S(1)}, bf16[96,2048]{1,0:T(8,128)(2,1)}, u32[]{:S(2)}, u32[]{:S(2)}) collective-permute-start(bf16[96,2048]{1,0:T(8,128)(2,1)S(1)} %constant_dynamic-slice_fusion.refs_9_), channel_id=1, source_target_pairs={{0,6},{1,7},{2,0},{3,1},{4,2},{5,3},{6,4},{7,5},{8,14},{9,15},{10,... | collective-permute-start | bytes 1179656 | tf_op jit(solution)/shard_map/ppermute | solution.py:138
  3.5 42.2 %collective-permute-start = (bf16[128,2048]{1,0:T(8,128)(2,1)}, bf16[128,2048]{1,0:T(8,128)(2,1)S(1)}, u32[]{:S(2)}, u32[]{:S(2)}) collective-permute-start(bf16[128,2048]{1,0:T(8,128)(2,1)} %refs_1_.3), channel_id=1, source_target_pairs={{0,8},{8,0},{16,24},{24,16},{1,9},{9,1},{17,25},{25,17},{2,10},{10... | collective-permute-start | bytes 1572872 | tf_op jit(solution)/shard_map/ppermute | solution.py:144
  5.0 40.7 %collective-permute-start.9 = (bf16[96,2048]{1,0:T(8,128)(2,1)S(1)}, bf16[96,2048]{1,0:T(8,128)(2,1)}, u32[]{:S(2)}, u32[]{:S(2)}) collective-permute-start(bf16[96,2048]{1,0:T(8,128)(2,1)S(1)} %constant_dynamic-slice_fusion.refs_9_), channel_id=1, source_target_pairs={{0,1},{1,0},{2,3},{3,2},{4,5},{5,4},{6,7},{7,6},{8,9},{9,8},{10,11... | collective-permute-start | bytes 1179656 | tf_op jit(solution)/shard_map/ppermute | solution.py:141
  19.8 26.4 %collective-permute-start.7 = (bf16[96,2048]{1,0:T(8,128)(2,1)}, bf16[96,2048]{1,0:T(8,128)(2,1)}, u32[]{:S(2)}, u32[]{:S(2)}) collective-permute-start(bf16[96,2048]{1,0:T(8,128)(2,1)} %collective-permute-done.6.refs_13_), channel_id=1, source_target_pairs={{0,2},{1,3},{2,4},{3,5},{4,6},{5,7},{6,0},{7,1},{8,10},{9,11},{10,... | collective-permute-start | bytes 1179656 | tf_op jit(solution)/shard_map/ppermute | solution.py:138
  22.5 16.4 %copy-start.5 = (s32[128,2]{1,0:T(8,128)}, s32[128,2]{1,0:T(8,128)S(1)}, u32[]{:S(2)}) copy-start(s32[128,2]{1,0:T(8,128)S(1)} %copy.16.refs_5_) | copy-start | bytes 3076
  22.5 4.3 %collective-permute-start.3 = (s32[128,2]{1,0:T(8,128)S(1)}, s32[128,2]{1,0:T(8,128)S(1)}, u32[]{:S(2)}, u32[]{:S(2)}) collective-permute-start(s32[128,2]{1,0:T(8,128)S(1)} %copy.16.refs_5_), channel_id=1, source_target_pairs={{0,8},{8,0},{16,24},{24,16},{1,9},{9,1},{17,25},{25,17},{2,10},{10... | collective-permute-start | bytes 3080 | tf_op jit(solution)/shard_map/ppermute | solution.py:144
  26.9 12.0 %copy-start.6 = (s32[128,2]{1,0:T(8,128)}, s32[128,2]{1,0:T(8,128)S(1)}, u32[]{:S(2)}) copy-start(s32[128,2]{1,0:T(8,128)S(1)} %collective-permute-done.3.refs_6_) | copy-start | bytes 3076
  26.9 10.6 %collective-permute-start.4 = (s32[128,2]{1,0:T(8,128)S(1)}, s32[128,2]{1,0:T(8,128)S(1)}, u32[]{:S(2)}, u32[]{:S(2)}) collective-permute-start(s32[128,2]{1,0:T(8,128)S(1)} %copy.16.refs_5_), channel_id=1, source_target_pairs={{0,16},{8,24},{16,0},{24,8},{1,17},{9,25},{17,1},{25,9},{2,18},{10... | collective-permute-start | bytes 3080 | tf_op jit(solution)/shard_map/ppermute | solution.py:144
  37.4 1.5 %copy-start.7 = (s32[128,2]{1,0:T(8,128)}, s32[128,2]{1,0:T(8,128)S(1)}, u32[]{:S(2)}) copy-start(s32[128,2]{1,0:T(8,128)S(1)} %collective-permute-done.4.refs_7_) | copy-start | bytes 3076
  37.4 5.3 %collective-permute-start.5 = (s32[128,2]{1,0:T(8,128)S(1)}, s32[128,2]{1,0:T(8,128)}, u32[]{:S(2)}, u32[]{:S(2)}) collective-permute-start(s32[128,2]{1,0:T(8,128)S(1)} %copy.16.refs_5_), channel_id=1, source_target_pairs={{0,24},{8,16},{16,8},{24,0},{1,25},{9,17},{17,9},{25,1},{2,26},{10... | collective-permute-start | bytes 3080 | tf_op jit(solution)/shard_map/ppermute | solution.py:144
  42.7 15.0 %collective-permute-start.1 = (bf16[128,2048]{1,0:T(8,128)(2,1)}, bf16[128,2048]{1,0:T(8,128)(2,1)S(1)}, u32[]{:S(2)}, u32[]{:S(2)}) collective-permute-start(bf16[128,2048]{1,0:T(8,128)(2,1)} %refs_1_.3), channel_id=1, source_target_pairs={{0,16},{8,24},{16,0},{24,8},{1,17},{9,25},{17,1},{25,9},{2,18},{10... | collective-permute-start | bytes 1572872 | tf_op jit(solution)/shard_map/ppermute | solution.py:144
  43.3 14.5 %collective-permute-start.2 = (bf16[128,2048]{1,0:T(8,128)(2,1)}, bf16[128,2048]{1,0:T(8,128)(2,1)S(1)}, u32[]{:S(2)}, u32[]{:S(2)}) collective-permute-start(bf16[128,2048]{1,0:T(8,128)(2,1)} %refs_1_.3), channel_id=1, source_target_pairs={{0,24},{8,16},{16,8},{24,0},{1,25},{9,17},{17,9},{25,1},{2,26},{10... | collective-permute-start | bytes 1572872 | tf_op jit(solution)/shard_map/ppermute | solution.py:144
  45.7 12.1 %collective-permute-start.12 = (bf16[96,2048]{1,0:T(8,128)(2,1)}, bf16[96,2048]{1,0:T(8,128)(2,1)}, u32[]{:S(2)}, u32[]{:S(2)}) collective-permute-start(bf16[96,2048]{1,0:T(8,128)(2,1)} %collective-permute-done.6.refs_13_), channel_id=1, source_target_pairs={{0,1},{1,0},{2,3},{3,2},{4,5},{5,4},{6,7},{7,6},{8,9},{9,8},{10,11... | collective-permute-start | bytes 1179656 | tf_op jit(solution)/shard_map/ppermute | solution.py:141
  45.7 12.1 %copy-start.1 = (bf16[128,2048]{1,0:T(8,128)(2,1)}, bf16[128,2048]{1,0:T(8,128)(2,1)S(1)}, u32[]{:S(2)}) copy-start(bf16[128,2048]{1,0:T(8,128)(2,1)S(1)} %collective-permute-done.refs_2_) | copy-start | bytes 1572868
  45.7 12.0 %collective-permute-start.11 = (bf16[96,2048]{1,0:T(8,128)(2,1)}, bf16[96,2048]{1,0:T(8,128)(2,1)}, u32[]{:S(2)}, u32[]{:S(2)}) collective-permute-start(bf16[96,2048]{1,0:T(8,128)(2,1)} %collective-permute-done.10.refs_11_), channel_id=1, source_target_pairs={{0,1},{1,0},{2,3},{3,2},{4,5},{5,4},{6,7},{7,6},{8,9},{9,8},{10,11... | collective-permute-start | bytes 1179656 | tf_op jit(solution)/shard_map/ppermute | solution.py:141
  46.2 19.0 %collective-permute-start.8 = (bf16[96,2048]{1,0:T(8,128)(2,1)}, bf16[96,2048]{1,0:T(8,128)(2,1)}, u32[]{:S(2)}, u32[]{:S(2)}) collective-permute-start(bf16[96,2048]{1,0:T(8,128)(2,1)} %collective-permute-done.7.refs_9_), channel_id=1, source_target_pairs={{0,1},{1,0},{2,3},{3,2},{4,5},{5,4},{6,7},{7,6},{8,9},{9,8},{10,11... | collective-permute-start | bytes 1179656 | tf_op jit(solution)/shard_map/ppermute | solution.py:141
  57.7 0.8 copy-start.2
  57.7 1.0 %copy-start.3 = (bf16[128,2048]{1,0:T(8,128)(2,1)}, bf16[128,2048]{1,0:T(8,128)(2,1)S(1)}, u32[]{:S(2)}) copy-start(bf16[128,2048]{1,0:T(8,128)(2,1)S(1)} %collective-permute-done.2.refs_4_) | copy-start | bytes 1572868
  69.1 4.8 %collective-permute-start.13 = (bf16[128,384]{1,0:T(8,128)(2,1)}, bf16[128,384]{1,0:T(8,128)(2,1)S(1)}, u32[]{:S(2)}, u32[]{:S(2)}) collective-permute-start(bf16[128,384]{1,0:T(8,128)(2,1)} %get-tuple-element.18), channel_id=1, source_target_pairs={{0,8},{8,0},{16,24},{24,16},{1,9},{9,1},{17,25},{25,17},{2,10},{10... | collective-permute-start | bytes 294920 | tf_op jit(solution)/shard_map/ppermute | solution.py:144
  70.6 4.8 %collective-permute-start.14 = (bf16[128,384]{1,0:T(8,128)(2,1)}, bf16[128,384]{1,0:T(8,128)(2,1)S(1)}, u32[]{:S(2)}, u32[]{:S(2)}) collective-permute-start(bf16[128,384]{1,0:T(8,128)(2,1)} %get-tuple-element.19), channel_id=1, source_target_pairs={{0,16},{8,24},{16,0},{24,8},{1,17},{9,25},{17,1},{25,9},{2,18},{10... | collective-permute-start | bytes 294920 | tf_op jit(solution)/shard_map/ppermute | solution.py:144
  71.2 5.7 %collective-permute-start.15 = (bf16[128,384]{1,0:T(8,128)(2,1)}, bf16[128,384]{1,0:T(8,128)(2,1)S(1)}, u32[]{:S(2)}, u32[]{:S(2)}) collective-permute-start(bf16[128,384]{1,0:T(8,128)(2,1)} %get-tuple-element.20), channel_id=1, source_target_pairs={{0,24},{8,16},{16,8},{24,0},{1,25},{9,17},{17,9},{25,1},{2,26},{10... | collective-permute-start | bytes 294920 | tf_op jit(solution)/shard_map/ppermute | solution.py:144
  78.7 0.7 copy-start.8
